TPU v7x, 256 devices: a whole 4x4x8 slice. The times are simulated.
256 devices in a mesh: dp: 8 (over z), task: 16 (over y, x), mp: 2 (over core).
Axes of the slice: x: 4, y: 4, z: 8, core: 2. Of those that a mesh axis runs over, the one named last changes fastest.
Arguments:
- deltas: bfloat16 [16, 2, 256, 28672], P('task', None, 'dp', 'mp'), may hold values from -3.984375 to 3.984375, as said below
- keep_blocks: int32 [16, 2, 2], P('task'), may hold values 0 or 1
- base_weights: bfloat16 [2, 256, 28672], P(None, 'dp', 'mp'), may hold values from -6 to 6
Outputs:
- merged: float32 [2, 256, 28672], P(None, 'dp', 'mp')
Inputs may be any that keep to these rules, and one draw needn't show every extreme that they name: `deltas`: every entry is a whole multiple of 1/64.
All inputs are finite; a program needn't handle non-finite values. No bound on the sum of `keep_blocks` on one device may be relied on, other than what follows from the above.
Results may differ from a plain program's by a relative error of at most 0.0003.
Values may be sent and summed in bfloat16 or wider, within the bound.
A program may use at most 128 MiB of HBM per device.

v0:
```python
import jax
import jax.numpy as jnp
from jax import lax
from jax.sharding import PartitionSpec as P

BLOCK = 128


def in_blocks(value, dim, devices):
    lengths = value.shape
    pieces = value.reshape(*lengths[:dim], devices, lengths[dim] // devices, *lengths[dim + 1 :])
    return jnp.moveaxis(pieces, dim, 0)


def cut_rows(length, count):
    unit = 8 if length >= 8 * count else 1
    return [length // unit * k // count * unit for k in range(1, count)]


def laid_out(pieces, dim):
    lengths = list(pieces.shape[1:])
    lengths[dim] *= pieces.shape[0]
    return jnp.moveaxis(pieces, 0, dim).reshape(lengths)


def exchange_in_pieces(value, axis, pieces, split_dim, concat_dim):
    blocks = in_blocks(value, split_dim, lax.axis_size(axis))
    widest = max(range(1, max(2, blocks.ndim - 1)), key=lambda d: blocks.shape[d])
    finished = []
    for slab in jnp.split(blocks, cut_rows(blocks.shape[widest], pieces), axis=widest):
        if slab.size:
            finished.append(lax.all_to_all(slab, axis, split_axis=0, concat_axis=0, tiled=True))
    return laid_out(jnp.concatenate(finished, axis=widest), concat_dim)


def combine(totals, own_base):
    upward, downward, up_count, down_count = totals
    elected = jnp.sign(upward + downward)
    upper_mean = upward / jnp.maximum(up_count, 1.0)
    lower_mean = downward / jnp.maximum(down_count, 1.0)
    agreed = jnp.where(elected > 0, upper_mean, jnp.where(elected < 0, lower_mean, 0.0))
    return own_base.astype(jnp.float32) + agreed


def statistics(trimmed):
    upward = jnp.maximum(trimmed, 0.0)
    downward = jnp.minimum(trimmed, 0.0)
    up_count = (trimmed > 0).astype(jnp.float32)
    down_count = (trimmed < 0).astype(jnp.float32)
    return (upward, downward, up_count, down_count)


def on_device(deltas, keep_blocks, base_weights):
    row_count = deltas.shape[2]
    block_count = keep_blocks.shape[2]
    row_start = lax.axis_index("dp") * row_count
    block_of_row = (row_start + jnp.arange(row_count, dtype=jnp.int32)) // BLOCK
    block_hits = (
        block_of_row[:, None] == jnp.arange(block_count, dtype=jnp.int32)[None, :]
    ).astype(jnp.float32)
    row_keep = jnp.dot(keep_blocks[0].astype(jnp.float32), block_hits.T)
    trimmed = deltas[0].astype(jnp.float32) * row_keep[:, :, None]
    share_rows = row_count // lax.axis_size("task")
    sendable = trimmed.astype(jnp.bfloat16)[None]
    arrived = exchange_in_pieces(sendable, "task", 2, 2, 0)
    upward, downward, up_count, down_count = statistics(arrived.astype(jnp.float32))
    totals = (
        jnp.sum(upward, axis=0),
        jnp.sum(downward, axis=0),
        jnp.sum(up_count, axis=0),
        jnp.sum(down_count, axis=0),
    )
    own_base = lax.dynamic_slice_in_dim(
        base_weights, lax.axis_index("task") * share_rows, share_rows, 1
    )
    merged_part = combine(totals, own_base)
    return lax.all_gather(merged_part, "task", axis=1, tiled=True)


def solution(mesh):
    in_specs = (P("task", None, "dp", "mp"), P("task", None, None), P(None, "dp", "mp"))
    out_specs = P(None, "dp", "mp")
    return jax.shard_map(
        on_device, mesh=mesh, in_specs=in_specs, out_specs=out_specs, check_vma=False
    )
```

profile of v0, /device:TPU:1, one launch (start us, length us, event | category | flops | bytes accessed | tf_op | source)
XLA Modules:
  0.0 137.9 jit_solution(14409906547524525671)
XLA Ops:
  6.5 0.9 convolution_bitcast_fusion
  7.4 0.1 copy.19
  7.5 3.4 %copy.13 = f32[1,2,32,14336]{3,1,2,0:T(2,128)S(1)} copy(bf16[1,2,32,14336]{3,2,1,0:T(8,128)(2,1)} %param.3) | data formatting | bytes 5505024 | tf_op jit(solution)/shard_map/convert_element_type | solution.py:62
  10.9 1.6 %fusion.4 = bf16[16,1,2,2,14336]{4,2,3,0,1:T(2,128)(2,1)S(1)} fusion(f32[1,2,16,2,14336]{4,1,3,2,0:T(2,128)S(1)} %bitcast.9, f32[2,16,2]{0,2,1:T(2,128)S(1)} %bitcast.10), kind=kLoop, calls=%fused_computation.9 | loop fusion | flops 1835008 | bytes 5505280 | tf_op jit(solution)/shard_map/transpose | solution.py:12
  12.5 3.9 %fusion.8 = (bf16[16,1,1,2,14336]{4,2,3,0,1:T(2,128)(2,1)S(1)}, bf16[16,1,1,2,14336]{4,2,3,0,1:T(2,128)(2,1)S(1)}) fusion(bf16[16,1,2,2,14336]{4,2,3,0,1:T(2,128)(2,1)S(1)} %fusion.4), kind=kLoop, calls=%fused_computation.24 | loop fusion | bytes 3670016 | tf_op jit(solution)/shard_map/split | solution.py:30
  16.4 1.9 %copy.15 = bf16[16,1,1,2,14336]{4,3,2,1,0:T(2,128)(2,1)} copy(bf16[16,1,1,2,14336]{4,2,3,0,1:T(2,128)(2,1)S(1)} %get-tuple-element.9) | data formatting | bytes 1835008 | tf_op jit(solution)/shard_map/split | solution.py:30
  18.3 7.6 %all-to-all-start = ((bf16[16,1,1,2,14336]{4,3,2,1,0:T(2,128)(2,1)}), bf16[16,1,1,2,14336]{4,3,2,1,0:T(2,128)(2,1)S(1)}, u32[]{:S(2)}, u32[]{:S(2)}) async-start(bf16[16,1,1,2,14336]{4,3,2,1,0:T(2,128)(2,1)} %copy.15), calls=%async_computation | async-start | bytes 1835008 | tf_op jit(solution)/shard_map/all_to_all | solution.py:32
  25.9 1.9 %copy.16 = bf16[16,1,1,2,14336]{4,3,2,1,0:T(2,128)(2,1)} copy(bf16[16,1,1,2,14336]{4,2,3,0,1:T(2,128)(2,1)S(1)} %get-tuple-element.10) | data formatting | bytes 1835008 | tf_op jit(solution)/shard_map/split | solution.py:30
  27.8 12.8 %all-to-all-done = bf16[16,1,1,2,14336]{4,3,2,1,0:T(2,128)(2,1)S(1)} async-done(((bf16[16,1,1,2,14336]{4,3,2,1,0:T(2,128)(2,1)}), bf16[16,1,1,2,14336]{4,3,2,1,0:T(2,128)(2,1)S(1)}, u32[]{:S(2)}, u32[]{:S(2)}) %all-to-all-start) | async-done | bytes 917536 | tf_op jit(solution)/shard_map/all_to_all | solution.py:32
  40.5 4.0 %all-to-all-start.1 = ((bf16[16,1,1,2,14336]{4,3,2,1,0:T(2,128)(2,1)}), bf16[16,1,1,2,14336]{4,3,2,1,0:T(2,128)(2,1)S(1)}, u32[]{:S(2)}, u32[]{:S(2)}) async-start(bf16[16,1,1,2,14336]{4,3,2,1,0:T(2,128)(2,1)} %copy.16), calls=%async_computation.1 | async-start | bytes 1835008 | tf_op jit(solution)/shard_map/all_to_all | solution.py:32
  44.5 0.2 all-gather.2.cloned.1.call-start
  44.7 13.6 %all-to-all-done.1 = bf16[16,1,1,2,14336]{4,3,2,1,0:T(2,128)(2,1)S(1)} async-done(((bf16[16,1,1,2,14336]{4,3,2,1,0:T(2,128)(2,1)}), bf16[16,1,1,2,14336]{4,3,2,1,0:T(2,128)(2,1)S(1)}, u32[]{:S(2)}, u32[]{:S(2)}) %all-to-all-start.1) | async-done | bytes 917536 | tf_op jit(solution)/shard_map/all_to_all | solution.py:32
  58.3 8.4 %fusion.2 = (f32[2,2,14336]{2,1,0:T(2,128)S(1)}, f32[2,2,14336]{2,1,0:T(2,128)S(1)}, f32[2,2,14336]{2,1,0:T(2,128)S(1)}, f32[2,2,14336]{2,1,0:T(2,128)S(1)}) fusion(bf16[16,1,1,2,14336]{4,3,2,1,0:T(2,128)(2,1)S(1)} %all-to-all-done.1, bf16[16,1,1,2,14336]{4,3,2,1,0:T(2,128)(2,1)S(1)} %all-to-all-done), kind=kLoop, calls=%fused_computation.6 | loop fusion | flops 10780672 | bytes 2752512 | tf_op jit(solution)/shard_map/reduce_sum | solution.py:70
  66.7 1.7 %convert_add_fusion = f32[2,2,14336]{2,1,0:T(2,128)S(1)} fusion(f32[2,2,14336]{2,1,0:T(2,128)S(1)} %get-tuple-element.6, f32[2,2,14336]{2,1,0:T(2,128)S(1)} %get-tuple-element.7, f32[2,2,14336]{2,1,0:T(2,128)S(1)} %get-tuple-element.8, f32[2,2,14336]{2,1,0:T(2,128)S(1)} %get-tuple-element.5, bf16[2,32,14336]{2,1,0:T(8,128)(2,1)} %param.5, s32[]{:T(128)S(6)} %select_n.20), kind=kLoop, calls=%fused_computation.15 | loop fusion | flops 688128 | bytes 1261572 | tf_op jit(solution)/shard_map/add | solution.py:42
  68.4 0.9 copy.17
  69.2 0.0 all-gather.2.cloned.1.call-update
  69.2 55.8 %all-gather.2.cloned.1.call-done = f32[2,32,14336]{2,0,1:T(2,128)} async-done(((f32[2,2,14336]{2,0,1:T(2,128)}), f32[2,32,14336]{2,0,1:T(2,128)}) %all-gather.2.cloned.1.call-update) | async-done | bytes 3670032 | tf_op jit(solution)/shard_map/all_gather | solution.py:77
  125.1 6.0 %copy.18 = f32[2,32,14336]{2,1,0:T(8,128)} copy(f32[2,32,14336]{2,0,1:T(2,128)} %all-gather.2.cloned.1.call-done) | data formatting | bytes 7340032 | tf_op jit(solution)/shard_map/all_gather | solution.py:77
  (1 shorter events, 0.0 us)
Async XLA Ops:
  18.3 22.2 %all-to-all-start = ((bf16[16,1,1,2,14336]{4,3,2,1,0:T(2,128)(2,1)}), bf16[16,1,1,2,14336]{4,3,2,1,0:T(2,128)(2,1)S(1)}, u32[]{:S(2)}, u32[]{:S(2)}) async-start(bf16[16,1,1,2,14336]{4,3,2,1,0:T(2,128)(2,1)} %copy.15), calls=%async_computation | async-start | bytes 1835008 | tf_op jit(solution)/shard_map/all_to_all | solution.py:32
  40.5 17.8 %all-to-all-start.1 = ((bf16[16,1,1,2,14336]{4,3,2,1,0:T(2,128)(2,1)}), bf16[16,1,1,2,14336]{4,3,2,1,0:T(2,128)(2,1)S(1)}, u32[]{:S(2)}, u32[]{:S(2)}) async-start(bf16[16,1,1,2,14336]{4,3,2,1,0:T(2,128)(2,1)} %copy.16), calls=%async_computation.1 | async-start | bytes 1835008 | tf_op jit(solution)/shard_map/all_to_all | solution.py:32
  44.5 80.6 %all-gather.2.cloned.1.call-start = ((), (), s32[]{:S(2)}) async-start(), calls=%async_computation.2 | async-start | bytes 3899392 | tf_op jit(solution)/shard_map/all_gather | solution.py:77
Sparse Core Ops, SparseCore 0:
  69.4 55.6 all-gather.1
where the time goes:
time: 138 us
  waiting for transfers between devices  82.2 us (60%)
  local copies, waits for them, and re-layouts  18 us (13%)
  between operations  13.5 us (10%)
  starting transfers between devices  11.8 us (9%)
  other arithmetic  11.7 us (8%)
    all_gather x1, waiting for transfers between devices, on_device(): return lax.all_gather(merged_part, 'task', axis=1, tiled=True)  55.8 us
    all_to_all x2, waiting for transfers between devices, exchange_in_pieces(): lax.all_to_all(slab, axis, split_axis=0, concat_axis=0, tiled=True)  26.3 us
    all_to_all x2, starting transfers between devices, exchange_in_pieces(): lax.all_to_all(slab, axis, split_axis=0, concat_axis=0, tiled=True)  11.5 us
    reduce_sum x1, other arithmetic, on_device(): jnp.sum(up_count, axis=0)  8.36 us
    split x3, local copies, waits for them, and re-layouts, exchange_in_pieces(): jnp.split(blocks, cut_rows(blocks.shape[widest], pieces), axis=widest)  7.63 us
    all_gather x1, local copies, waits for them, and re-layouts, on_device(): return lax.all_gather(merged_part, 'task', axis=1, tiled=True)  6 us
    convert_element_type x1, local copies, waits for them, and re-layouts, on_device(): trimmed = deltas[0].astype(jnp.float32) * row_keep[:, :, None]  3.39 us
  transfers between devices with their start and end apart: 3, of which 3 were waited for; matrix products, arithmetic and copies ran while one was open for 1% of the time, Pallas kernels for 0%

commit v1 on v0

--- a/solution.py
+++ b/solution.py
@@ -4,6 +4,11 @@
 from jax.sharding import PartitionSpec as P
 
 BLOCK = 128
+
+
+def gather_from_all(array, axis, dim):
+    copies = jnp.concatenate([array] * lax.axis_size(axis), axis=dim)
+    return lax.all_to_all(copies, axis, dim, dim, tiled=True)
 
 
 def in_blocks(value, dim, devices):
@@ -74,7 +79,7 @@
         base_weights, lax.axis_index("task") * share_rows, share_rows, 1
     )
     merged_part = combine(totals, own_base)
-    return lax.all_gather(merged_part, "task", axis=1, tiled=True)
+    return gather_from_all(merged_part, "task", 1)
 
 
 def solution(mesh):

time: 138 us -> 128 us (0.928); the launches traced: 138 us -> 126 us
  waiting for transfers between devices: 82.2 us -> 26.6 us
  blocking collectives: 0 us -> 48.1 us
  between operations: 13.5 us -> 0.06 us
  local copies, waits for them, and re-layouts: 18 us -> 27.6 us
    all_gather x1 -> x0, waiting for transfers between devices: 55.8 us -> none  [on_device(): return lax.all_gather(merged_part, 'task', axis=1, tiled=True)]
    all_to_all x0 -> x1, blocking collectives: none -> 48.1 us  [gather_from_all(): return lax.all_to_all(copies, axis, dim, dim, tiled=True)]
    concatenate x0 -> x2, local copies, waits for them, and re-layouts: none -> 12.5 us  [gather_from_all(): copies = jnp.concatenate([array] * lax.axis_size(axis), axis=dim)]
    all_gather x1 -> x0, local copies, waits for them, and re-layouts: 6 us -> none  [on_device(): return lax.all_gather(merged_part, 'task', axis=1, tiled=True)]
    all_to_all x0 -> x1, local copies, waits for them, and re-layouts: none -> 3.96 us  [gather_from_all(): return lax.all_to_all(copies, axis, dim, dim, tiled=True)]
  transfers between devices with their start and end apart: 3 -> 2, of which waited for: 3 -> 2; matrix products, arithmetic and copies ran while one was open for 1% -> 1% of each run, Pallas kernels for 0% -> 0%
where the time goes in v1:
time: 128 us; the launch traced here: 126 us
  blocking collectives  48.1 us (38%)
  local copies, waits for them, and re-layouts  27.6 us (22%)
  waiting for transfers between devices  26.6 us (21%)
  other arithmetic  11.7 us (9%)
  starting transfers between devices  11.5 us (9%)
    all_to_all x1, blocking collectives, gather_from_all(): return lax.all_to_all(copies, axis, dim, dim, tiled=True)  48.1 us
    all_to_all x2, waiting for transfers between devices, exchange_in_pieces(): lax.all_to_all(slab, axis, split_axis=0, concat_axis=0, tiled=True)  26.6 us
    concatenate x2, local copies, waits for them, and re-layouts, gather_from_all(): copies = jnp.concatenate([array] * lax.axis_size(axis), axis=dim)  12.5 us
    all_to_all x2, starting transfers between devices, exchange_in_pieces(): lax.all_to_all(slab, axis, split_axis=0, concat_axis=0, tiled=True)  11.5 us
    reduce_sum x1, other arithmetic, on_device(): jnp.sum(up_count, axis=0)  8.36 us
    split x3, local copies, waits for them, and re-layouts, exchange_in_pieces(): jnp.split(blocks, cut_rows(blocks.shape[widest], pieces), axis=widest)  7.63 us
    all_to_all x1, local copies, waits for them, and re-layouts, gather_from_all(): return lax.all_to_all(copies, axis, dim, dim, tiled=True)  3.96 us
    convert_element_type x1, local copies, waits for them, and re-layouts, on_device(): trimmed = deltas[0].astype(jnp.float32) * row_keep[:, :, None]  3.39 us
  transfers between devices with their start and end apart: 2, of which 2 were waited for; matrix products, arithmetic and copies ran while one was open for 1% of the time, Pallas kernels for 0%

profile of v1, /device:TPU:1, one launch (start us, length us, event | category | flops | bytes accessed | tf_op | source)
XLA Modules:
  0.0 126.4 jit_solution(18187136601568411969)
XLA Ops:
  0.0 0.9 convolution_bitcast_fusion
  0.9 0.1 copy.19
  1.0 3.4 %copy.13 = f32[1,2,32,14336]{3,1,2,0:T(2,128)S(1)} copy(bf16[1,2,32,14336]{3,2,1,0:T(8,128)(2,1)} %param.3) | data formatting | bytes 5505024 | tf_op jit(solution)/shard_map/convert_element_type | solution.py:67
  4.4 1.6 %fusion.4 = bf16[16,1,2,2,14336]{4,2,3,0,1:T(2,128)(2,1)S(1)} fusion(f32[1,2,16,2,14336]{4,1,3,2,0:T(2,128)S(1)} %bitcast.9, f32[2,16,2]{0,2,1:T(2,128)S(1)} %bitcast.10), kind=kLoop, calls=%fused_computation.9 | loop fusion | flops 1835008 | bytes 5505280 | tf_op jit(solution)/shard_map/transpose | solution.py:17
  6.0 3.9 %fusion.8 = (bf16[16,1,1,2,14336]{4,2,3,0,1:T(2,128)(2,1)S(1)}, bf16[16,1,1,2,14336]{4,2,3,0,1:T(2,128)(2,1)S(1)}) fusion(bf16[16,1,2,2,14336]{4,2,3,0,1:T(2,128)(2,1)S(1)} %fusion.4), kind=kLoop, calls=%fused_computation.24 | loop fusion | bytes 3670016 | tf_op jit(solution)/shard_map/split | solution.py:35
  9.9 1.9 %copy.15 = bf16[16,1,1,2,14336]{4,3,2,1,0:T(2,128)(2,1)} copy(bf16[16,1,1,2,14336]{4,2,3,0,1:T(2,128)(2,1)S(1)} %get-tuple-element.9) | data formatting | bytes 1835008 | tf_op jit(solution)/shard_map/split | solution.py:35
  11.8 7.6 %all-to-all-start = ((bf16[16,1,1,2,14336]{4,3,2,1,0:T(2,128)(2,1)}), bf16[16,1,1,2,14336]{4,3,2,1,0:T(2,128)(2,1)S(1)}, u32[]{:S(2)}, u32[]{:S(2)}) async-start(bf16[16,1,1,2,14336]{4,3,2,1,0:T(2,128)(2,1)} %copy.15), calls=%async_computation | async-start | bytes 1835008 | tf_op jit(solution)/shard_map/all_to_all | solution.py:37
  19.4 1.9 %copy.16 = bf16[16,1,1,2,14336]{4,3,2,1,0:T(2,128)(2,1)} copy(bf16[16,1,1,2,14336]{4,2,3,0,1:T(2,128)(2,1)S(1)} %get-tuple-element.10) | data formatting | bytes 1835008 | tf_op jit(solution)/shard_map/split | solution.py:35
  21.2 12.8 %all-to-all-done = bf16[16,1,1,2,14336]{4,3,2,1,0:T(2,128)(2,1)S(1)} async-done(((bf16[16,1,1,2,14336]{4,3,2,1,0:T(2,128)(2,1)}), bf16[16,1,1,2,14336]{4,3,2,1,0:T(2,128)(2,1)S(1)}, u32[]{:S(2)}, u32[]{:S(2)}) %all-to-all-start) | async-done | bytes 917536 | tf_op jit(solution)/shard_map/all_to_all | solution.py:37
  34.0 4.0 %all-to-all-start.1 = ((bf16[16,1,1,2,14336]{4,3,2,1,0:T(2,128)(2,1)}), bf16[16,1,1,2,14336]{4,3,2,1,0:T(2,128)(2,1)S(1)}, u32[]{:S(2)}, u32[]{:S(2)}) async-start(bf16[16,1,1,2,14336]{4,3,2,1,0:T(2,128)(2,1)} %copy.16), calls=%async_computation.1 | async-start | bytes 1835008 | tf_op jit(solution)/shard_map/all_to_all | solution.py:37
  38.0 13.8 %all-to-all-done.1 = bf16[16,1,1,2,14336]{4,3,2,1,0:T(2,128)(2,1)S(1)} async-done(((bf16[16,1,1,2,14336]{4,3,2,1,0:T(2,128)(2,1)}), bf16[16,1,1,2,14336]{4,3,2,1,0:T(2,128)(2,1)S(1)}, u32[]{:S(2)}, u32[]{:S(2)}) %all-to-all-start.1) | async-done | bytes 917536 | tf_op jit(solution)/shard_map/all_to_all | solution.py:37
  51.8 8.4 %fusion.2 = (f32[2,2,14336]{2,1,0:T(2,128)S(1)}, f32[2,2,14336]{2,1,0:T(2,128)S(1)}, f32[2,2,14336]{2,1,0:T(2,128)S(1)}, f32[2,2,14336]{2,1,0:T(2,128)S(1)}) fusion(bf16[16,1,1,2,14336]{4,3,2,1,0:T(2,128)(2,1)S(1)} %all-to-all-done.1, bf16[16,1,1,2,14336]{4,3,2,1,0:T(2,128)(2,1)S(1)} %all-to-all-done), kind=kLoop, calls=%fused_computation.6 | loop fusion | flops 10780672 | bytes 2752512 | tf_op jit(solution)/shard_map/reduce_sum | solution.py:75
  60.1 1.7 %convert_add_fusion = f32[2,2,14336]{2,1,0:T(2,128)S(1)} fusion(f32[2,2,14336]{2,1,0:T(2,128)S(1)} %get-tuple-element.6, f32[2,2,14336]{2,1,0:T(2,128)S(1)} %get-tuple-element.7, f32[2,2,14336]{2,1,0:T(2,128)S(1)} %get-tuple-element.8, f32[2,2,14336]{2,1,0:T(2,128)S(1)} %get-tuple-element.5, bf16[2,32,14336]{2,1,0:T(8,128)(2,1)} %param.5, s32[]{:T(128)S(6)} %select_n.20), kind=kLoop, calls=%fused_computation.15 | loop fusion | flops 688128 | bytes 1261572 | tf_op jit(solution)/shard_map/add | solution.py:47
  61.8 7.6 %concatenate.7 = f32[2,32,14336]{2,1,0:T(8,128)} concatenate(f32[2,2,14336]{2,1,0:T(2,128)S(1)} %convert_add_fusion, f32[2,2,14336]{2,1,0:T(2,128)S(1)} %convert_add_fusion, f32[2,2,14336]{2,1,0:T(2,128)S(1)} %convert_add_fusion, f32[2,2,14336]{2,1,0:T(2,128)S(1)} %convert_add_fusion, f32[2,2,14336]{2,1,0:T(2,128)S(1)} %convert_add_fusion, f32[2,2,14336]{2,1,0:T(2,128)S(1)} %convert_add_fusion, ...), dimensions={1} | concatenate | bytes 7340032 | tf_op jit(solution)/shard_map/concatenate | solution.py:10
  69.5 4.9 %copy.17 = f32[2,32,14336]{2,0,1:T(2,128)S(1)} copy(f32[2,32,14336]{2,1,0:T(8,128)} %concatenate.7) | data formatting | bytes 7340032 | tf_op jit(solution)/shard_map/concatenate | solution.py:10
  74.3 48.1 %all_to_all.15 = f32[2,32,14336]{2,0,1:T(2,128)S(1)} all-to-all(f32[2,32,14336]{2,0,1:T(2,128)S(1)} %copy.17), channel_id=1, replica_groups=mesh['dp'=8,'task'=16,'mp'=2] {'task'}, dimensions={1} | all-to-all | bytes 7340032 | tf_op jit(solution)/shard_map/all_to_all | solution.py:11
  122.4 4.0 %copy.18 = f32[2,32,14336]{2,1,0:T(8,128)} copy(f32[2,32,14336]{2,0,1:T(2,128)S(1)} %all_to_all.15) | data formatting | bytes 7340032 | tf_op jit(solution)/shard_map/all_to_all | solution.py:11
  (1 shorter events, 0.0 us)
Async XLA Ops:
  11.8 22.2 %all-to-all-start = ((bf16[16,1,1,2,14336]{4,3,2,1,0:T(2,128)(2,1)}), bf16[16,1,1,2,14336]{4,3,2,1,0:T(2,128)(2,1)S(1)}, u32[]{:S(2)}, u32[]{:S(2)}) async-start(bf16[16,1,1,2,14336]{4,3,2,1,0:T(2,128)(2,1)} %copy.15), calls=%async_computation | async-start | bytes 1835008 | tf_op jit(solution)/shard_map/all_to_all | solution.py:37
  34.0 17.8 %all-to-all-start.1 = ((bf16[16,1,1,2,14336]{4,3,2,1,0:T(2,128)(2,1)}), bf16[16,1,1,2,14336]{4,3,2,1,0:T(2,128)(2,1)S(1)}, u32[]{:S(2)}, u32[]{:S(2)}) async-start(bf16[16,1,1,2,14336]{4,3,2,1,0:T(2,128)(2,1)} %copy.16), calls=%async_computation.1 | async-start | bytes 1835008 | tf_op jit(solution)/shard_map/all_to_all | solution.py:37
